TPU v7x, 256 devices: a whole 4x4x8 slice. The times are simulated.
256 devices in a mesh: row: 32 (over x, z_lo, core), chan: 8 (over y, z_hi).
Axes of the slice: x: 4, y: 4, z: 8 (z_hi: 2, z_lo: 4; z = z_hi * 4 + z_lo), core: 2. Of those that a mesh axis runs over, the one named last changes fastest.
Arguments:
- pair: bfloat16 [128, 768, 768], P('chan', 'row'), may hold values from -24 to 24
- single: bfloat16 [768, 384], P('row'), may hold values from -6 to 6
- token_mask: int32 [768], replicated, may hold values from 0 to 1, as said below
- pair_gain: float32 [128], replicated, may hold values from 0.5 to 1.5
- w_ab: bfloat16 [128, 4, 128], replicated, may hold values from -0.5 to 0.5
- w_out_gate: bfloat16 [128, 128], replicated, may hold values from -0.5 to 0.5
- x_gain: float32 [128], replicated, may hold values from 0.5 to 1.5
- w_tri_out: bfloat16 [128, 128], replicated, may hold values from -0.5 to 0.5
- bias_gain: float32 [128], replicated, may hold values from 0.5 to 1.5
- w_bias: bfloat16 [128, 16], replicated, may hold values from -0.5 to 0.5
- single_gain: float32 [384], replicated, may hold values from 0.5 to 1.5
- w_query: bfloat16 [384, 384], P(None, 'chan'), may hold values from -1 to 1
- w_key: bfloat16 [384, 384], P(None, 'chan'), may hold values from -16 to 16
- w_value_gate: bfloat16 [384, 2, 384], P(None, None, 'chan'), may hold values from -0.3125 to 0.3125
- w_mix: bfloat16 [384, 384], P('chan'), may hold values from -0.3125 to 0.3125
Outputs:
- pair_out: bfloat16 [128, 768, 768], P('chan', 'row')
- attended: bfloat16 [768, 384], P('row', 'chan')
Inputs may be any that keep to these rules, and one draw needn't show every extreme that they name: token_mask is 1 on the first tokens and 0 on the rest; at least 672 tokens are real.
All inputs are finite; a program needn't handle non-finite values.
Results may differ from a plain program's by a relative error of at most 0.015.
The roundings to bfloat16 on the way count: a program that leaves them out, or rounds other values in their place, can miss the bound.
Values may be sent and summed in bfloat16 or wider, within the bound.
No kernel may reach another device: no remote copies, remote signals or barrier semaphores. Data moves between devices by JAX's collectives and lax.ppermute only.
A program may use at most 64 MiB of HBM per device.

v0:
```python
import jax
import jax.numpy as jnp
from jax import lax
from jax.sharding import Mesh
from jax.sharding import PartitionSpec as P

D = 384
H = 16
CHAN = ("chan_0", "chan_1")
EPS = 1e-05


def gathered_by_axis(shard, axes, dim):
    for axis in reversed(axes):
        shard = lax.all_gather(shard, axis, axis=dim, tiled=True)
    return shard


def sent_together(arrays, axis, dim, along):
    widths = [a.shape[along] for a in arrays]
    both = jnp.concatenate(arrays, axis=along)
    whole = lax.all_gather(both, axis, axis=dim, tiled=True)
    return tuple(jnp.split(whole, [sum(widths[:k]) for k in range(1, len(widths))], axis=along))


def cut_along(shard, dim, peers):
    before, after = (shard.shape[:dim], shard.shape[dim + 1 :])
    return jnp.moveaxis(shard.reshape(*before, peers, -1, *after), dim, 0)


def sent_and_summed(shard, axis, dim):
    peers = lax.axis_size(axis)
    blocks = lax.all_to_all(cut_along(shard, dim, peers), axis, 0, 0, tiled=True)
    return jnp.sum(blocks.astype(jnp.float32), axis=0)


def layer_norm(values, gain, axis):
    middle = jnp.mean(values, axis=axis, keepdims=True)
    centred = values - middle
    spread = jnp.mean(centred * centred, axis=axis, keepdims=True)
    return centred * lax.rsqrt(spread + EPS) * gain


def body(
    pair,
    single,
    token_mask,
    pair_gain,
    w_ab,
    w_out_gate,
    x_gain,
    w_tri_out,
    bias_gain,
    w_bias,
    single_gain,
    w_query,
    w_key,
    w_value_gate,
    w_mix,
):
    chans = pair.shape[0]
    rows = pair.shape[1]
    width = pair.shape[2]
    ranks = lax.axis_size("row")
    chan_start = lax.axis_index(CHAN) * chans
    row_start = lax.axis_index("row") * rows
    live = token_mask.astype(jnp.float32)
    live_rows = lax.dynamic_slice_in_dim(live, row_start, rows, 0)
    pair_mask = live_rows[:, None] * live[None, :]
    full = gathered_by_axis(pair, CHAN, 0)
    normed = layer_norm(full.astype(jnp.float32), pair_gain[:, None, None], 0).astype(jnp.bfloat16)
    w_own = lax.dynamic_slice_in_dim(w_ab, chan_start, chans, 2)
    share = max(1, ranks // chans)
    per_owner = max(1, chans // ranks)
    groups = chans // per_owner
    part_rows = rows // share
    projected = jnp.einsum("cik,cpd->pdik", normed, w_own, preferred_element_type=jnp.float32)
    left = (jax.nn.sigmoid(projected[0]) * projected[1] * pair_mask[None]).astype(jnp.bfloat16)
    right = (jax.nn.sigmoid(projected[2]) * projected[3] * pair_mask[None]).astype(jnp.bfloat16)
    left_send = left.reshape(groups, per_owner, share, part_rows, width).transpose(0, 2, 1, 3, 4)
    left_send = left_send.reshape(ranks * per_owner, part_rows, width)
    right_send = jnp.broadcast_to(
        right.reshape(groups, 1, per_owner, rows, width), (groups, share, per_owner, rows, width)
    )
    right_send = right_send.reshape(ranks * per_owner, rows, width)
    left_owned, right_owned = (
        lax.all_to_all(left_send, "row", split_axis=0, concat_axis=1, tiled=True),
        lax.all_to_all(right_send, "row", split_axis=0, concat_axis=1, tiled=True),
    )
    owned = jnp.einsum(
        "uik,ujk->uij", left_owned, right_owned, preferred_element_type=jnp.float32
    ).astype(jnp.bfloat16)
    returned = lax.all_to_all(owned, "row", split_axis=1, concat_axis=0, tiled=True)
    summed = (
        returned.reshape(groups, share, per_owner, part_rows, width)
        .transpose(0, 2, 1, 3, 4)
        .reshape(chans, rows, width)
    )
    crossed = lax.all_gather(summed, CHAN, axis=0, tiled=True)
    product_normed = layer_norm(crossed.astype(jnp.float32), x_gain[:, None, None], 0).astype(
        jnp.bfloat16
    )
    out_gate = jax.nn.sigmoid(
        jnp.einsum("cij,cd->dij", normed, w_out_gate, preferred_element_type=jnp.float32)
    )
    update = jnp.einsum(
        "cij,cd->dij", product_normed, w_tri_out, preferred_element_type=jnp.float32
    )
    renewed = (full.astype(jnp.float32) + out_gate * update).astype(jnp.bfloat16)
    pair_out = lax.dynamic_slice_in_dim(renewed, chan_start, chans, 0)
    head_size = D // H
    local_width = w_query.shape[1]
    heads = local_width // head_size
    head_start = lax.axis_index(CHAN) * heads
    bias_input = layer_norm(renewed.astype(jnp.float32), bias_gain[:, None, None], 0).astype(
        jnp.bfloat16
    )
    w_bias_own = lax.dynamic_slice_in_dim(w_bias, head_start, heads, 1)
    bias = jnp.einsum("cij,ch->hij", bias_input, w_bias_own, preferred_element_type=jnp.float32)
    single_normed = layer_norm(single.astype(jnp.float32), single_gain[None, :], 1).astype(
        jnp.bfloat16
    )
    queries = jnp.dot(single_normed, w_query, preferred_element_type=jnp.float32).astype(
        jnp.bfloat16
    )
    head_gate = jax.nn.sigmoid(
        jnp.dot(single_normed, w_value_gate[:, 1, :], preferred_element_type=jnp.float32)
    )
    own_keys = jnp.dot(single_normed, w_key, preferred_element_type=jnp.float32).astype(
        jnp.bfloat16
    )
    own_values = jnp.dot(
        single_normed, w_value_gate[:, 0, :], preferred_element_type=jnp.float32
    ).astype(jnp.bfloat16)
    keys, values = sent_together((own_keys, own_values), "row", 0, 1)
    tokens = keys.shape[0]
    query_heads = queries.reshape(rows, heads, head_size)
    key_heads = keys.reshape(tokens, heads, head_size)
    value_heads = values.reshape(tokens, heads, head_size)
    scores = jnp.einsum("ihe,jhe->hij", query_heads, key_heads, preferred_element_type=jnp.float32)
    scores = scores / jnp.sqrt(jnp.float32(head_size)) + bias
    scores = jnp.where(live[None, None, :] > 0, scores, -jnp.inf)
    top = jnp.max(scores, axis=2, keepdims=True)
    raised = jnp.exp(scores - top)
    weights = (raised / jnp.sum(raised, axis=2, keepdims=True)).astype(jnp.bfloat16)
    mixed = jnp.einsum("hij,jhe->ihe", weights, value_heads, preferred_element_type=jnp.float32)
    heads_out = (mixed.reshape(rows, local_width) * head_gate).astype(jnp.bfloat16)
    terms = jnp.dot(heads_out, w_mix, preferred_element_type=jnp.float32)
    attended = sent_and_summed(terms.astype(jnp.bfloat16), CHAN, 1).astype(jnp.bfloat16)
    return (pair_out, attended)


def solution(mesh):
    split = Mesh(mesh.devices.reshape(mesh.shape["row"], 4, 2), ("row", "chan_0", "chan_1"))
    return jax.shard_map(
        body,
        mesh=split,
        in_specs=(
            P(CHAN, "row", None),
            P("row", None),
            P(),
            P(),
            P(),
            P(),
            P(),
            P(),
            P(),
            P(),
            P(),
            P(None, CHAN),
            P(None, CHAN),
            P(None, None, CHAN),
            P(CHAN, None),
        ),
        out_specs=(P(CHAN, "row", None), P("row", CHAN)),
        check_vma=False,
    )
```

profile of v0, /device:TPU:2, one launch (start us, length us, event | category | flops | bytes accessed | tf_op | source)
XLA Modules:
  0.0 371.6 jit_solution(35078988886564830)
XLA Ops:
  7.2 2.0 copy.73
  9.3 48.9 %all-gather.4.cloned.1.call-done = bf16[32,24,768]{2,0,1:T(8,128)(2,1)} async-done(((bf16[16,24,768]{2,0,1:T(8,128)(2,1)}), bf16[32,24,768]{2,0,1:T(8,128)(2,1)}) %all-gather.4.cloned.1.call-update) | async-done | bytes 1179664 | tf_op jit(solution)/shard_map/all_gather | solution.py:15
  58.5 0.7 convert_element_type.70
  59.6 51.7 %all-gather.6.cloned.1.call-done = bf16[128,24,768]{2,0,1:T(8,128)(2,1)} async-done(((bf16[32,24,768]{2,0,1:T(8,128)(2,1)}), bf16[128,24,768]{2,0,1:T(8,128)(2,1)}) %all-gather.6.cloned.1.call-update) | async-done | bytes 4718608 | tf_op jit(solution)/shard_map/all_gather | solution.py:15
  111.3 3.2 convert_reduce_fusion
  114.5 0.5 copy-done.1
  115.0 1.4 fusion.7
  116.4 1.9 fusion.17
  118.4 2.2 copy-done.3
  120.6 0.3 slice_multiply_fusion.1
  120.9 1.7 copy.76
  122.6 1.4 reshape.164
  123.9 1.1 multiply_convert_fusion
  125.0 7.9 %all-to-all-start = ((bf16[32,12,768]{2,1,0:T(8,128)(2,1)}), bf16[32,12,768]{2,1,0:T(8,128)(2,1)S(1)}, u32[]{:S(2)}, u32[]{:S(2)}) async-start(bf16[32,12,768]{2,1,0:T(8,128)(2,1)} %multiply_convert_fusion), calls=%async_computation | async-start | bytes 1572864 | tf_op jit(solution)/shard_map/all_to_all | solution.py:87
  132.9 2.0 fusion.26
  135.1 17.5 %all-to-all-done = bf16[32,12,768]{2,1,0:T(8,128)(2,1)S(1)} async-done(((bf16[32,12,768]{2,1,0:T(8,128)(2,1)}), bf16[32,12,768]{2,1,0:T(8,128)(2,1)S(1)}, u32[]{:S(2)}, u32[]{:S(2)}) %all-to-all-start) | async-done | bytes 589856 | tf_op jit(solution)/shard_map/all_to_all | solution.py:87
  152.6 1.1 broadcast_in_dim.12
  153.8 6.4 %all-to-all-start.1 = ((bf16[32,24,768]{2,1,0:T(8,128)(2,1)}), bf16[32,24,768]{2,1,0:T(8,128)(2,1)S(1)}, u32[]{:S(2)}, u32[]{:S(2)}) async-start(bf16[32,24,768]{2,1,0:T(8,128)(2,1)} %bitcast.5), calls=%async_computation.1 | async-start | bytes 2359296 | tf_op jit(solution)/shard_map/all_to_all | solution.py:88
  160.2 0.2 all-gather.8.cloned.1.call-start
  160.5 27.7 %all-to-all-done.1 = bf16[32,24,768]{2,1,0:T(8,128)(2,1)S(1)} async-done(((bf16[32,24,768]{2,1,0:T(8,128)(2,1)}), bf16[32,24,768]{2,1,0:T(8,128)(2,1)S(1)}, u32[]{:S(2)}, u32[]{:S(2)}) %all-to-all-start.1) | async-done | bytes 1179680 | tf_op jit(solution)/shard_map/all_to_all | solution.py:88
  188.3 0.7 fusion.23
  189.0 0.9 copy.105
  189.9 0.5 broadcast.172
  190.4 4.2 %reduce.1 = bf16[384,768]{1,0:T(8,128)(2,1)S(1)} reduce(bf16[384,1,768]{2,1,0:T(2,128)(2,1)S(1)} %bitcast.64, bf16[]{:T(256)} %broadcast.172), dimensions={1}, to_apply=%bitcast.61.reduce_sub_computation | reduce | bytes 1179650
  194.7 0.2 reshape.171
  194.9 21.7 %all_to_all.32 = bf16[32,2,4608]{2,1,0:T(2,128)(2,1)S(1)} all-to-all(bf16[32,2,4608]{2,1,0:T(2,128)(2,1)S(1)} %reshape.171), channel_id=1, replica_groups=mesh['row'=32,'chan_0'=4,'chan_1'=2] {'row'}, dimensions={0} | all-to-all | bytes 1179648 | tf_op jit(solution)/shard_map/all_to_all | solution.py:93
  216.6 0.5 reshape.172
  217.1 0.9 copy.94
  218.4 0.2 convolution_convert_fusion.3
  218.9 38.8 %all_gather.15 = bf16[768,96]{1,0:T(8,128)(2,1)S(1)} all-gather(bf16[24,96]{1,0:T(8,128)(2,1)S(1)} %pad_maximum_fusion), channel_id=1, replica_groups=mesh['row'=32,'chan_0'=4,'chan_1'=2] {'row'}, dimensions={0}, use_global_device_ids=true | all-gather | bytes 152064 | tf_op jit(solution)/shard_map/all_gather | solution.py:22
  257.9 0.2 convolution_convert_fusion.2
  258.4 73.8 %all-gather.8.cloned.1.call-done = bf16[128,24,768]{2,1,0:T(8,128)(2,1)} async-done(((bf16[16,24,768]{2,1,0:T(8,128)(2,1)}), bf16[128,24,768]{2,1,0:T(8,128)(2,1)}) %all-gather.8.cloned.1.call-update) | async-done | bytes 4718608 | tf_op jit(solution)/shard_map/all_gather | solution.py:99
  332.2 3.2 convert_reduce_fusion.2
  335.4 0.6 copy-done.2
  335.9 1.3 fusion.13
  337.2 1.4 fusion.15
  338.7 1.4 fusion.19
  340.2 5.2 %convert_reduce_fusion.1 = (f32[24,768]{1,0:T(8,128)S(1)}, bf16[128,24,768]{2,0,1:T(8,128)(2,1)S(1)}) fusion(f32[24,768,128]{1,2,0:T(8,128)S(1)} %fusion.19, bf16[128,128]{1,0:T(8,128)(2,1)S(1)} %copy-done.14, bf16[128,24,768]{2,0,1:T(8,128)(2,1)S(1)} %bitcast.63, f32[128]{0:T(128)S(1)} %copy-done.9, f32[24,768]{1,0:T(8,128)S(1)} %add_rsqrt_fusion.2, ...), kind=kOutput, calls=%fused_computation.5 | convolution fusion | flops 636991488 | bytes 19128832 | tf_op jit(solution)/shard_map/cij,cd->dij/dot_general | solution.py:104
  345.5 1.3 fusion.10
  346.9 2.3 fusion.21
  349.5 0.2 fusion.44
  349.8 0.4 convolution_convert_fusion.1
  350.3 0.7 reshape.173
  351.0 3.3 all-to-all-start.3
  354.3 1.1 constant_dynamic-slice_fusion.1
  355.4 1.0 copy.88
  356.4 7.9 %all-to-all-done.3 = bf16[8,2,576]{2,1,0:T(2,128)(2,1)S(1)} async-done(((bf16[8,2,576]{2,1,0:T(2,128)(2,1)}), bf16[8,2,576]{2,1,0:T(2,128)(2,1)S(1)}, u32[]{:S(2)}, u32[]{:S(2)}) %all-to-all-start.3) | async-done | bytes 18464 | tf_op jit(solution)/shard_map/all_to_all | solution.py:33
  364.5 0.6 reduce_sum.102
  (72 shorter events, 2.9 us)
Async XLA Ops:
  7.2 51.1 %copy-start = (bf16[128,4,128]{2,1,0:T(4,128)(2,1)S(1)}, bf16[128,4,128]{2,1,0:T(4,128)(2,1)}, u32[]{:S(2)}) copy-start(bf16[128,4,128]{2,1,0:T(4,128)(2,1)} %param.19) | copy-start | bytes 393220
  7.2 51.0 %all-gather.4.cloned.1.call-start = ((), (), s32[]{:S(2)}) async-start(), calls=%async_computation.4 | async-start | bytes 1769472 | tf_op jit(solution)/shard_map/all_gather | solution.py:15
  9.3 102.0 %all-gather.6.cloned.1.call-start = ((), (), s32[]{:S(2)}) async-start(), calls=%async_computation.5 | async-start | bytes 5898240 | tf_op jit(solution)/shard_map/all_gather | solution.py:15
  59.5 56.9 %copy-start.9 = (f32[128]{0:T(128)S(1)}, f32[128]{0:T(128)}, u32[]{:S(2)}) copy-start(f32[128]{0:T(128)} %param.18) | copy-start | bytes 1540
  111.3 3.8 %copy-start.1 = (bf16[128,24,768]{2,0,1:T(8,128)(2,1)S(1)}, bf16[128,24,768]{2,0,1:T(8,128)(2,1)}, u32[]{:S(2)}) copy-start(bf16[128,24,768]{2,0,1:T(8,128)(2,1)} %all-gather.6.cloned.1.call-done) | copy-start | bytes 14155780
  118.4 2.2 copy-start.3
  125.0 27.6 %all-to-all-start = ((bf16[32,12,768]{2,1,0:T(8,128)(2,1)}), bf16[32,12,768]{2,1,0:T(8,128)(2,1)S(1)}, u32[]{:S(2)}, u32[]{:S(2)}) async-start(bf16[32,12,768]{2,1,0:T(8,128)(2,1)} %multiply_convert_fusion), calls=%async_computation | async-start | bytes 1572864 | tf_op jit(solution)/shard_map/all_to_all | solution.py:87
  153.8 34.5 %all-to-all-start.1 = ((bf16[32,24,768]{2,1,0:T(8,128)(2,1)}), bf16[32,24,768]{2,1,0:T(8,128)(2,1)S(1)}, u32[]{:S(2)}, u32[]{:S(2)}) async-start(bf16[32,24,768]{2,1,0:T(8,128)(2,1)} %bitcast.5), calls=%async_computation.1 | async-start | bytes 2359296 | tf_op jit(solution)/shard_map/all_to_all | solution.py:88
  160.2 172.0 %all-gather.8.cloned.1.call-start = ((), (), s32[]{:S(2)}) async-start(), calls=%async_computation.6 | async-start | bytes 5308416 | tf_op jit(solution)/shard_map/all_gather | solution.py:99
  189.0 29.1 %copy-start.5 = (bf16[24,384]{1,0:T(8,128)(2,1)S(1)}, bf16[24,384]{1,0:T(8,128)(2,1)}, u32[]{:S(2)}) copy-start(bf16[24,384]{1,0:T(8,128)(2,1)} %param.16) | copy-start | bytes 55300
  189.0 29.4 %copy-start.10 = (bf16[384,2,48]{0,2,1:T(8,128)(2,1)S(1)}, bf16[384,2,48]{0,2,1:T(8,128)(2,1)}, u32[]{:S(2)}) copy-start(bf16[384,2,48]{0,2,1:T(8,128)(2,1)} %param.28) | copy-start | bytes 221188
  189.0 29.4 %copy-start.15 = (f32[384]{0:T(512)S(1)}, f32[384]{0:T(512)}, u32[]{:S(2)}) copy-start(f32[384]{0:T(512)} %param.25) | copy-start | bytes 4612
  189.0 29.6 %copy-start.11 = (bf16[384,48]{0,1:T(8,128)(2,1)S(1)}, bf16[384,48]{0,1:T(8,128)(2,1)}, u32[]{:S(2)}) copy-start(bf16[384,48]{0,1:T(8,128)(2,1)} %param.27) | copy-start | bytes 110596
  190.4 67.5 %copy-start.12 = (bf16[384,48]{0,1:T(8,128)(2,1)S(1)}, bf16[384,48]{0,1:T(8,128)(2,1)}, u32[]{:S(2)}) copy-start(bf16[384,48]{0,1:T(8,128)(2,1)} %param.26) | copy-start | bytes 110596
  190.4 67.9 %copy-start.7 = (s32[768]{0:T(1024)S(1)}, s32[768]{0:T(1024)}, u32[]{:S(2)}) copy-start(s32[768]{0:T(1024)} %param.17) | copy-start | bytes 9220
  258.3 78.9 %copy-start.8 = (f32[128]{0:T(128)S(1)}, f32[128]{0:T(128)}, u32[]{:S(2)}) copy-start(f32[128]{0:T(128)} %param.21) | copy-start | bytes 1540
  332.2 3.8 %copy-start.2 = (bf16[128,24,768]{2,1,0:T(8,128)(2,1)S(1)}, bf16[128,24,768]{2,1,0:T(8,128)(2,1)}, u32[]{:S(2)}) copy-start(bf16[128,24,768]{2,1,0:T(8,128)(2,1)} %all-gather.8.cloned.1.call-done) | copy-start | bytes 14155780
  337.2 1.5 copy-start.6
  337.2 2.9 slice-start
  338.7 1.5 slice-start.1
  338.7 1.5 copy-start.14
  345.4 3.7 copy-start.4
  345.4 1.4 copy-start.16
  346.9 2.9 copy-start.13
  351.0 13.4 %all-to-all-start.3 = ((bf16[8,2,576]{2,1,0:T(2,128)(2,1)}), bf16[8,2,576]{2,1,0:T(2,128)(2,1)S(1)}, u32[]{:S(2)}, u32[]{:S(2)}) async-start(bf16[8,2,576]{2,1,0:T(2,128)(2,1)} %reshape.173), calls=%async_computation.3 | async-start | bytes 40960 | tf_op jit(solution)/shard_map/all_to_all | solution.py:33
Sparse Core Ops, SparseCore 0:
  10.4 47.7 all-gather.3
  60.0 51.2 all-gather.5
  218.2 113.9 all-gather.7
where the time goes:
time: 372 us
  waiting for transfers between devices  228 us (61%)
  blocking collectives  60.5 us (16%)
  other arithmetic  21.5 us (6%)
  starting transfers between devices  17.9 us (5%)
  local copies, waits for them, and re-layouts  17 us (5%)
  between operations  14.2 us (4%)
  matrix products  12.9 us (3%)
    all_gather x2, waiting for transfers between devices, gathered_by_axis(): shard = lax.all_gather(shard, axis, axis=dim, tiled=True)  101 us
    all_gather x1, waiting for transfers between devices, body(): crossed = lax.all_gather(summed, CHAN, axis=0, tiled=True)  73.8 us
    all_gather x1, blocking collectives, sent_together(): whole = lax.all_gather(both, axis, axis=dim, tiled=True)  38.8 us
    all_to_all x1, waiting for transfers between devices, body(): lax.all_to_all(right_send, 'row', split_axis=0, concat_axis=1, tiled=True)  27.7 us
    all_to_all x1, blocking collectives, body(): lax.all_to_all(owned, 'row', split_axis=1, concat_axis=0, tiled=True)  21.7 us
    all_to_all x1, waiting for transfers between devices, body(): lax.all_to_all(left_send, 'row', split_axis=0, concat_axis=1, tiled=True)  17.5 us
    unnamed x47, local copies, waits for them, and re-layouts  9.37 us
    all_to_all x1, waiting for transfers between devices, sent_and_summed(): lax.all_to_all(cut_along(shard, dim, peers), axis, 0, 0, tiled=True)  7.95 us
  transfers between devices with their start and end apart: 6, of which 6 were waited for; matrix products, arithmetic and copies ran while one was open for 2% of the time, Pallas kernels for 0%

commit v1 on v0

--- a/solution.py
+++ b/solution.py
@@ -96,7 +96,9 @@
         .transpose(0, 2, 1, 3, 4)
         .reshape(chans, rows, width)
     )
-    crossed = lax.all_gather(summed, CHAN, axis=0, tiled=True)
+    crossed = jnp.concatenate(
+        lax.all_to_all(jnp.stack([summed] * lax.axis_size(CHAN)), CHAN, 0, 0), axis=0
+    )
     product_normed = layer_norm(crossed.astype(jnp.float32), x_gain[:, None, None], 0).astype(
         jnp.bfloat16
     )

time: 372 us -> 420 us (1.13); the launches traced: 372 us -> 413 us
  blocking collectives: 60.5 us -> 155 us
  waiting for transfers between devices: 228 us -> 154 us
  starting transfers between devices: 17.9 us -> 28.7 us
  other arithmetic: 21.5 us -> 28.4 us
    all_gather x1, blocking collectives: 38.8 us -> 133 us  [sent_together(): whole = lax.all_gather(both, axis, axis=dim, tiled=True)]
    all_gather x1 -> x0, waiting for transfers between devices: 73.8 us -> none  [body(): crossed = lax.all_gather(summed, CHAN, axis=0, tiled=True)]
    all_to_all x0 -> x1, starting transfers between devices: none -> 6.03 us  [body(): lax.all_to_all(jnp.stack([summed] * lax.axis_size(CHAN)), CHAN, 0, 0)]
    all_to_all x1, starting transfers between devices: 3.31 us -> 8.22 us  [sent_and_summed(): lax.all_to_all(cut_along(shard, dim, peers), axis, 0, 0, tiled=True)]
  transfers between devices with their start and end apart: 6 -> 6, of which waited for: 6 -> 5; matrix products, arithmetic and copies ran while one was open for 2% -> 2% of each run, Pallas kernels for 0% -> 0%
where the time goes in v1:
time: 420 us; the launch traced here: 413 us
  blocking collectives  155 us (37%)
  waiting for transfers between devices  154 us (37%)
  starting transfers between devices  28.7 us (7%)
  other arithmetic  28.4 us (7%)
  local copies, waits for them, and re-layouts  19 us (5%)
  between operations  14.5 us (3%)
  matrix products  13.4 us (3%)
    all_gather x1, blocking collectives, sent_together(): whole = lax.all_gather(both, axis, axis=dim, tiled=True)  133 us
    all_gather x2, waiting for transfers between devices, gathered_by_axis(): shard = lax.all_gather(shard, axis, axis=dim, tiled=True)  101 us
    all_to_all x1, waiting for transfers between devices, body(): lax.all_to_all(right_send, 'row', split_axis=0, concat_axis=1, tiled=True)  28 us
    all_to_all x1, blocking collectives, body(): lax.all_to_all(owned, 'row', split_axis=1, concat_axis=0, tiled=True)  21.7 us
    all_to_all x1, waiting for transfers between devices, body(): lax.all_to_all(left_send, 'row', split_axis=0, concat_axis=1, tiled=True)  17.6 us
    unnamed x47, local copies, waits for them, and re-layouts  8.73 us
  transfers between devices with their start and end apart: 6, of which 5 were waited for; matrix products, arithmetic and copies ran while one was open for 2% of the time, Pallas kernels for 0%

profile of v1, /device:TPU:2, one launch (start us, length us, event | category | flops | bytes accessed | tf_op | source)
XLA Modules:
  0.0 413.1 jit_solution(843195158555995870)
XLA Ops:
  7.2 2.0 copy.57
  9.3 48.9 %all-gather.3.cloned.1.call-done = bf16[32,24,768]{2,0,1:T(8,128)(2,1)} async-done(((bf16[16,24,768]{2,0,1:T(8,128)(2,1)}), bf16[32,24,768]{2,0,1:T(8,128)(2,1)}) %all-gather.3.cloned.1.call-update) | async-done | bytes 1179664 | tf_op jit(solution)/shard_map/all_gather | solution.py:15
  58.5 0.7 convert_element_type.77
  59.6 51.7 %all-gather.5.cloned.1.call-done = bf16[128,24,768]{2,0,1:T(8,128)(2,1)} async-done(((bf16[32,24,768]{2,0,1:T(8,128)(2,1)}), bf16[128,24,768]{2,0,1:T(8,128)(2,1)}) %all-gather.5.cloned.1.call-update) | async-done | bytes 4718608 | tf_op jit(solution)/shard_map/all_gather | solution.py:15
  111.3 3.2 convert_reduce_fusion
  114.5 0.5 copy-done.2
  115.0 1.4 fusion.5
  116.4 1.9 fusion.15
  118.4 2.2 copy-done.3
  120.6 0.3 slice_multiply_fusion.1
  120.9 1.7 copy.60
  122.6 1.4 reshape.169
  123.9 1.1 multiply_convert_fusion
  125.0 7.9 %all-to-all-start = ((bf16[32,12,768]{2,1,0:T(8,128)(2,1)}), bf16[32,12,768]{2,1,0:T(8,128)(2,1)S(1)}, u32[]{:S(2)}, u32[]{:S(2)}) async-start(bf16[32,12,768]{2,1,0:T(8,128)(2,1)} %multiply_convert_fusion), calls=%async_computation | async-start | bytes 1572864 | tf_op jit(solution)/shard_map/all_to_all | solution.py:87
  133.0 2.0 fusion.25
  135.1 17.6 %all-to-all-done = bf16[32,12,768]{2,1,0:T(8,128)(2,1)S(1)} async-done(((bf16[32,12,768]{2,1,0:T(8,128)(2,1)}), bf16[32,12,768]{2,1,0:T(8,128)(2,1)S(1)}, u32[]{:S(2)}, u32[]{:S(2)}) %all-to-all-start) | async-done | bytes 589856 | tf_op jit(solution)/shard_map/all_to_all | solution.py:87
  152.7 1.1 broadcast_in_dim.12
  153.8 6.4 %all-to-all-start.1 = ((bf16[32,24,768]{2,1,0:T(8,128)(2,1)}), bf16[32,24,768]{2,1,0:T(8,128)(2,1)S(1)}, u32[]{:S(2)}, u32[]{:S(2)}) async-start(bf16[32,24,768]{2,1,0:T(8,128)(2,1)} %bitcast.5), calls=%async_computation.1 | async-start | bytes 2359296 | tf_op jit(solution)/shard_map/all_to_all | solution.py:88
  160.4 28.0 %all-to-all-done.1 = bf16[32,24,768]{2,1,0:T(8,128)(2,1)S(1)} async-done(((bf16[32,24,768]{2,1,0:T(8,128)(2,1)}), bf16[32,24,768]{2,1,0:T(8,128)(2,1)S(1)}, u32[]{:S(2)}, u32[]{:S(2)}) %all-to-all-start.1) | async-done | bytes 1179680 | tf_op jit(solution)/shard_map/all_to_all | solution.py:88
  188.3 0.7 fusion.22
  189.0 0.9 copy.96
  189.9 0.5 broadcast.174
  190.4 4.2 %reduce.3 = bf16[384,768]{1,0:T(8,128)(2,1)S(1)} reduce(bf16[384,1,768]{2,1,0:T(2,128)(2,1)S(1)} %bitcast.72, bf16[]{:T(256)} %broadcast.174), dimensions={1}, to_apply=%bitcast.69.reduce_sub_computation | reduce | bytes 1179650
  194.6 0.2 reshape.177
  194.9 21.7 %all_to_all.37 = bf16[32,2,4608]{2,1,0:T(2,128)(2,1)S(1)} all-to-all(bf16[32,2,4608]{2,1,0:T(2,128)(2,1)S(1)} %reshape.177), channel_id=1, replica_groups=mesh['row'=32,'chan_0'=4,'chan_1'=2] {'row'}, dimensions={0} | all-to-all | bytes 1179648 | tf_op jit(solution)/shard_map/all_to_all | solution.py:93
  216.6 0.5 reshape.178
  217.3 2.6 stack.3
  220.0 6.0 %all-to-all-start.3 = ((bf16[8,16,24,768]{3,1,2,0:T(8,128)(2,1)}), bf16[8,16,24,768]{3,1,2,0:T(8,128)(2,1)}, u32[]{:S(2)}, u32[]{:S(2)}) async-start(bf16[8,16,24,768]{3,1,2,0:T(8,128)(2,1)} %stack.3), calls=%async_computation.3 | async-start | bytes 9437184 | tf_op jit(solution)/shard_map/all_to_all | solution.py:100
  226.5 0.2 convolution_convert_fusion.4
  226.8 133.1 %all_gather.11 = bf16[768,96]{1,0:T(8,128)(2,1)S(1)} all-gather(bf16[24,96]{1,0:T(8,128)(2,1)S(1)} %pad_maximum_fusion), channel_id=1, replica_groups=mesh['row'=32,'chan_0'=4,'chan_1'=2] {'row'}, dimensions={0}, use_global_device_ids=true | all-gather | bytes 152064 | tf_op jit(solution)/shard_map/all_gather | solution.py:22
  360.2 0.2 convolution_convert_fusion.2
  360.6 3.7 fusion.21
  364.3 4.1 multiply_reduce_fusion
  368.5 3.9 copy_convert_fusion
  372.4 1.2 fusion.14
  373.6 1.4 fusion.17
  375.0 0.7 slice-done.1
  375.8 5.6 %convert_reduce_fusion.1 = (f32[24,768]{1,0:T(8,128)S(1)}, bf16[128,24,768]{2,0,1:T(8,128)(2,1)S(1)}) fusion(f32[24,768,128]{1,2,0:T(8,128)S(1)} %fusion.17, bf16[128,128]{1,0:T(8,128)(2,1)S(1)} %copy-done.14, bf16[128,24,768]{2,0,1:T(8,128)(2,1)S(1)} %bitcast.71, f32[128]{0:T(128)S(1)} %copy-done.9, f32[24,768]{1,0:T(8,128)S(1)} %add_rsqrt_fusion.2, ...), kind=kOutput, calls=%fused_computation.5 | convolution fusion | flops 636991488 | bytes 19128832 | tf_op jit(solution)/shard_map/cij,cd->dij/dot_general | solution.py:106
  381.4 1.4 fusion.8
  382.9 2.4 fusion.19
  385.6 0.2 fusion.43
  385.9 0.4 convolution_convert_fusion.1
  386.4 0.7 reshape.179
  387.1 8.2 %all-to-all-start.4 = ((bf16[8,2,576]{2,1,0:T(2,128)(2,1)}), bf16[8,2,576]{2,1,0:T(2,128)(2,1)S(1)}, u32[]{:S(2)}, u32[]{:S(2)}) async-start(bf16[8,2,576]{2,1,0:T(2,128)(2,1)} %reshape.179), calls=%async_computation.4 | async-start | bytes 40960 | tf_op jit(solution)/shard_map/all_to_all | solution.py:33
  395.4 1.1 constant_dynamic-slice_fusion.1
  396.5 1.0 copy.74
  397.5 8.0 %all-to-all-done.4 = bf16[8,2,576]{2,1,0:T(2,128)(2,1)S(1)} async-done(((bf16[8,2,576]{2,1,0:T(2,128)(2,1)}), bf16[8,2,576]{2,1,0:T(2,128)(2,1)S(1)}, u32[]{:S(2)}, u32[]{:S(2)}) %all-to-all-start.4) | async-done | bytes 18464 | tf_op jit(solution)/shard_map/all_to_all | solution.py:33
  405.6 0.6 reduce_sum.102
  (74 shorter events, 3.1 us)
Async XLA Ops:
  7.2 51.1 %copy-start = (bf16[128,4,128]{2,1,0:T(4,128)(2,1)S(1)}, bf16[128,4,128]{2,1,0:T(4,128)(2,1)}, u32[]{:S(2)}) copy-start(bf16[128,4,128]{2,1,0:T(4,128)(2,1)} %param.19) | copy-start | bytes 393220
  7.2 51.0 %all-gather.3.cloned.1.call-start = ((), (), s32[]{:S(2)}) async-start(), calls=%async_computation.5 | async-start | bytes 1769472 | tf_op jit(solution)/shard_map/all_gather | solution.py:15
  9.3 102.0 %all-gather.5.cloned.1.call-start = ((), (), s32[]{:S(2)}) async-start(), calls=%async_computation.6 | async-start | bytes 5898240 | tf_op jit(solution)/shard_map/all_gather | solution.py:15
  59.5 56.9 %copy-start.9 = (f32[128]{0:T(128)S(1)}, f32[128]{0:T(128)}, u32[]{:S(2)}) copy-start(f32[128]{0:T(128)} %param.18) | copy-start | bytes 1540
  111.3 3.8 copy-start.2
  118.4 2.2 copy-start.3
  125.0 27.6 %all-to-all-start = ((bf16[32,12,768]{2,1,0:T(8,128)(2,1)}), bf16[32,12,768]{2,1,0:T(8,128)(2,1)S(1)}, u32[]{:S(2)}, u32[]{:S(2)}) async-start(bf16[32,12,768]{2,1,0:T(8,128)(2,1)} %multiply_convert_fusion), calls=%async_computation | async-start | bytes 1572864 | tf_op jit(solution)/shard_map/all_to_all | solution.py:87
  153.8 34.5 %all-to-all-start.1 = ((bf16[32,24,768]{2,1,0:T(8,128)(2,1)}), bf16[32,24,768]{2,1,0:T(8,128)(2,1)S(1)}, u32[]{:S(2)}, u32[]{:S(2)}) async-start(bf16[32,24,768]{2,1,0:T(8,128)(2,1)} %bitcast.5), calls=%async_computation.1 | async-start | bytes 2359296 | tf_op jit(solution)/shard_map/all_to_all | solution.py:88
  219.9 6.1 %copy-start.5 = (bf16[24,384]{1,0:T(8,128)(2,1)S(1)}, bf16[24,384]{1,0:T(8,128)(2,1)}, u32[]{:S(2)}) copy-start(bf16[24,384]{1,0:T(8,128)(2,1)} %param.16) | copy-start | bytes 55300
  219.9 6.4 %copy-start.10 = (bf16[384,2,48]{0,2,1:T(8,128)(2,1)S(1)}, bf16[384,2,48]{0,2,1:T(8,128)(2,1)}, u32[]{:S(2)}) copy-start(bf16[384,2,48]{0,2,1:T(8,128)(2,1)} %param.28) | copy-start | bytes 221188
  219.9 6.4 %copy-start.15 = (f32[384]{0:T(512)S(1)}, f32[384]{0:T(512)}, u32[]{:S(2)}) copy-start(f32[384]{0:T(512)} %param.25) | copy-start | bytes 4612
  219.9 6.6 %copy-start.11 = (bf16[384,48]{0,1:T(8,128)(2,1)S(1)}, bf16[384,48]{0,1:T(8,128)(2,1)}, u32[]{:S(2)}) copy-start(bf16[384,48]{0,1:T(8,128)(2,1)} %param.27) | copy-start | bytes 110596
  219.9 140.2 %copy-start.12 = (bf16[384,48]{0,1:T(8,128)(2,1)S(1)}, bf16[384,48]{0,1:T(8,128)(2,1)}, u32[]{:S(2)}) copy-start(bf16[384,48]{0,1:T(8,128)(2,1)} %param.26) | copy-start | bytes 110596
  220.0 140.6 %copy-start.7 = (s32[768]{0:T(1024)S(1)}, s32[768]{0:T(1024)}, u32[]{:S(2)}) copy-start(s32[768]{0:T(1024)} %param.17) | copy-start | bytes 9220
  220.0 140.6 %all-to-all-start.3 = ((bf16[8,16,24,768]{3,1,2,0:T(8,128)(2,1)}), bf16[8,16,24,768]{3,1,2,0:T(8,128)(2,1)}, u32[]{:S(2)}, u32[]{:S(2)}) async-start(bf16[8,16,24,768]{3,1,2,0:T(8,128)(2,1)} %stack.3), calls=%async_computation.3 | async-start | bytes 9437184 | tf_op jit(solution)/shard_map/all_to_all | solution.py:100
  368.4 3.9 copy-start.8
  372.3 1.2 copy-start.6
  372.3 2.7 slice-start
  373.6 2.2 slice-start.1
  373.6 2.2 copy-start.14
  381.4 3.9 copy-start.4
  381.4 1.4 copy-start.16
  382.8 23.4 %copy-start.1 = (bf16[128,4,128]{2,1,0:T(4,128)(2,1)S(1)}, bf16[128,4,128]{2,1,0:T(4,128)(2,1)}, u32[]{:S(2)}) copy-start(bf16[128,4,128]{2,1,0:T(4,128)(2,1)} %param.19) | copy-start | bytes 393220
  382.9 3.1 copy-start.13
  387.1 18.4 %all-to-all-start.4 = ((bf16[8,2,576]{2,1,0:T(2,128)(2,1)}), bf16[8,2,576]{2,1,0:T(2,128)(2,1)S(1)}, u32[]{:S(2)}, u32[]{:S(2)}) async-start(bf16[8,2,576]{2,1,0:T(2,128)(2,1)} %reshape.179), calls=%async_computation.4 | async-start | bytes 40960 | tf_op jit(solution)/shard_map/all_to_all | solution.py:33
Sparse Core Ops, SparseCore 0:
  10.4 47.7 all-gather.2
  60.0 51.2 all-gather.4
